TPU v7x, 32 devices: a whole 2x2x4 slice. The times are simulated.
32 devices in a mesh: rows: 8 (over z, x), width: 4 (over y, core).
Axes of the slice: x: 2, y: 2, z: 4, core: 2. Of those that a mesh axis runs over, the one named last changes fastest.
Arguments:
- weight_gate: float32 [2560, 9728], P('rows', 'width'), may hold values from -0.15625 to 0.15625
- moment_gate: float32 [2560, 9728], P('rows', 'width'), may hold values from -6 to 6
- square_gate: float32 [2560, 9728], P('rows', 'width'), may hold values from 0.1 to 10
- weight_up: float32 [2560, 9728], P('rows', 'width'), may hold values from -0.15625 to 0.15625
- moment_up: float32 [2560, 9728], P('rows', 'width'), may hold values from -6 to 6
- square_up: float32 [2560, 9728], P('rows', 'width'), may hold values from 0.1 to 10
- norm_gain: float32 [2560], P('rows'), may hold values from 0.25 to 1.75
Outputs:
- ready_gate: bfloat16 [2560, 9728], P(None, 'width')
- ready_up: bfloat16 [2560, 9728], P(None, 'width')
- column_gate: float32 [9728], P('width')
- column_up: float32 [9728], P('width')
All inputs are finite; a program needn't handle non-finite values.
Results may differ from a plain program's by a relative error of at most 0.0004.
Values may be sent and summed in bfloat16 or wider, within the bound.
A program may use at most 128 MiB of HBM per device.

v0:
```python
import jax
import jax.numpy as jnp
from jax import lax
from jax.sharding import PartitionSpec as P

learn_rate = 0.02
decay_rate = 0.1
tiny_value = 1e-08


def per_device(weight_gate, moment_gate, square_gate, weight_up, moment_up, square_up, norm_gain):
    latest_gate = weight_gate - learn_rate * (
        moment_gate / (jnp.sqrt(square_gate) + tiny_value) + decay_rate * weight_gate
    )
    latest_up = weight_up - learn_rate * (
        moment_up / (jnp.sqrt(square_up) + tiny_value) + decay_rate * weight_up
    )
    latest_gained_gate = latest_gate * norm_gain[:, None]
    latest_gained_up = latest_up * norm_gain[:, None]
    total_gate, total_up = lax.psum(
        (
            jnp.sum(latest_gained_gate * latest_gained_gate, axis=0),
            jnp.sum(latest_gained_up * latest_gained_up, axis=0),
        ),
        "rows",
    )
    column_gate = jnp.sqrt(total_gate)
    column_up = jnp.sqrt(total_up)
    narrow_gate, narrow_up = (
        (latest_gained_gate / column_gate).astype(jnp.bfloat16),
        (latest_gained_up / column_up).astype(jnp.bfloat16),
    )
    ready_gate, ready_up = (
        lax.all_gather(narrow_gate, "rows", axis=0, tiled=True),
        lax.all_gather(narrow_up, "rows", axis=0, tiled=True),
    )
    return (ready_gate, ready_up, column_gate, column_up)


def solution(mesh):
    in_specs = (
        P("rows", "width"),
        P("rows", "width"),
        P("rows", "width"),
        P("rows", "width"),
        P("rows", "width"),
        P("rows", "width"),
        P("rows"),
    )
    out_specs = (P(None, "width"), P(None, "width"), P("width"), P("width"))
    return jax.shard_map(
        per_device, mesh=mesh, in_specs=in_specs, out_specs=out_specs, check_vma=False
    )
```

profile of v0, /device:TPU:0, one launch (start us, length us, event | category | flops | bytes accessed | tf_op | source)
XLA Modules:
  0.0 430.4 jit_solution(8670219446207998635)
XLA Ops:
  7.2 0.0 all-gather.3.cloned.1.call-start
  7.2 9.3 %multiply_reduce_fusion = (f32[2432]{0:T(1024)S(1)}, f32[320,2432]{1,0:T(8,128)S(1)}, f32[2432]{0:T(1024)S(1)}, f32[320,2432]{1,0:T(8,128)}) fusion(f32[320]{0:T(512)} %param.13, f32[320,2432]{1,0:T(8,128)} %param.10, f32[320,2432]{1,0:T(8,128)} %param.11, f32[320,2432]{1,0:T(8,128)} %param.12, f32[320,2432]{1,0:T(8,128)} %param.7, f32[320,2432]{1,0:T(8,128)} %param.8, ...), kind=kLoop, calls=%fused_computation.1 | loop fusion | flops 14003456 | bytes 24924416 | tf_op jit(solution)/shard_map/reduce_sum | solution.py:23
  16.6 38.8 %all-reduce = (f32[2432]{0:T(1024)S(1)}, f32[2432]{0:T(1024)S(1)}) all-reduce(f32[2432]{0:T(1024)S(1)} %get-tuple-element.10, f32[2432]{0:T(1024)S(1)} %get-tuple-element.6), channel_id=1, replica_groups=mesh['rows'=8,'width'=4] {'rows'}, use_global_device_ids=true, to_apply=%region_1.0 | all-reduce | flops 4864 | bytes 38912 | tf_op jit(solution)/shard_map/psum | solution.py:20
  55.4 0.0 copy-start.1
  55.4 3.2 divide_convert_fusion.1
  58.6 0.0 all-gather.3.cloned.1.call-update
  58.6 0.0 copy-done.1
  58.7 0.0 all-gather.5.cloned.1.call-start
  58.7 0.0 copy-start.2
  58.7 1.3 divide_convert_fusion
  60.1 0.0 all-gather.5.cloned.1.call-update
  60.1 0.0 copy-done.2
  60.1 170.5 %all-gather.3.cloned.1.call-done = bf16[2560,2432]{1,0:T(8,128)(2,1)} async-done(((bf16[320,2432]{1,0:T(8,128)(2,1)}), bf16[2560,2432]{1,0:T(8,128)(2,1)}) %all-gather.3.cloned.1.call-update) | async-done | bytes 12451856 | tf_op jit(solution)/shard_map/all_gather | solution.py:34
  230.6 175.5 %all-gather.5.cloned.1.call-done = bf16[2560,2432]{1,0:T(8,128)(2,1)} async-done(((bf16[320,2432]{1,0:T(8,128)(2,1)}), bf16[2560,2432]{1,0:T(8,128)(2,1)}) %all-gather.5.cloned.1.call-update) | async-done | bytes 12451856 | tf_op jit(solution)/shard_map/all_gather | solution.py:35
  406.1 0.0 copy-start
  406.1 11.0 %copy.13 = bf16[2560,2432]{1,0:T(8,128)(2,1)} copy(bf16[2560,2432]{1,0:T(8,128)(2,1)} %all-gather.3.cloned.1.call-done) | data formatting | bytes 24903680
  417.1 1.8 copy-done
  418.8 4.7 %copy.14 = bf16[2560,2432]{1,0:T(8,128)(2,1)} copy(bf16[2560,2432]{1,0:T(8,128)(2,1)S(1)} %copy-done) | data formatting | bytes 24903680
  (2 shorter events, 0.0 us)
Async XLA Ops:
  7.2 223.4 %all-gather.3.cloned.1.call-start = ((), (), s32[]{:S(2)}) async-start(), calls=%async_computation | async-start | bytes 14008320 | tf_op jit(solution)/shard_map/all_gather | solution.py:34
  55.4 3.2 copy-start.1
  58.7 347.4 %all-gather.5.cloned.1.call-start = ((), (), s32[]{:S(2)}) async-start(), calls=%async_computation.1 | async-start | bytes 14008320 | tf_op jit(solution)/shard_map/all_gather | solution.py:35
  58.7 1.4 copy-start.2
  406.1 12.8 %copy-start = (bf16[2560,2432]{1,0:T(8,128)(2,1)S(1)}, bf16[2560,2432]{1,0:T(8,128)(2,1)}, u32[]{:S(2)}) copy-start(bf16[2560,2432]{1,0:T(8,128)(2,1)} %all-gather.5.cloned.1.call-done) | copy-start | bytes 37355524
Sparse Core Ops, SparseCore 0:
  58.8 171.7 all-gather.2
  233.3 172.6 all-gather.4
where the time goes:
time: 431 us; the launch traced here: 430 us
  waiting for transfers between devices  346 us (80%)
  blocking collectives  38.8 us (9%)
  local copies, waits for them, and re-layouts  17.5 us (4%)
  between operations  14.1 us (3%)
  other arithmetic  13.9 us (3%)
    all_gather x1, waiting for transfers between devices, per_device(): lax.all_gather(narrow_up, 'rows', axis=0, tiled=True)  175 us
    all_gather x1, waiting for transfers between devices, per_device(): lax.all_gather(narrow_gate, 'rows', axis=0, tiled=True)  170 us
    psum x1, blocking collectives, per_device(): lax.psum((jnp.sum(latest_gained_gate * latest_gained_gate, axis=0), jnp.s...  38.8 us
    unnamed x8, local copies, waits for them, and re-layouts  17.5 us
    reduce_sum x1, other arithmetic, per_device(): jnp.sum(latest_gained_up * latest_gained_up, axis=0)  9.34 us
  transfers between devices with their start and end apart: 2, of which 2 were waited for; matrix products, arithmetic and copies ran while one was open for 0% of the time, Pallas kernels for 0%

commit v1 on v0

v1 whole, which is shorter than its diff:
```python
import functools

import jax
import jax.numpy as jnp
from jax import lax
from jax.experimental import pallas as pl
from jax.experimental.pallas import tpu as pltpu
from jax.sharding import PartitionSpec as P

learn_rate = 0.02
decay_rate = 0.1
tiny_value = 1e-08
lanes = 128
block_rows = 16
MESH = pl.DeviceIdType.MESH


def column_cuts(columns):
    tiles = columns // lanes
    first = max(1, tiles // 9)
    rest = tiles - first
    sizes = [first] + [rest // 3 + (1 if i < rest % 3 else 0) for i in range(3)]
    cuts, at = [], 0
    for size in sizes:
        if size:
            cuts.append((at * lanes, size * lanes))
        at += size
    return cuts


def gather_kernel(
    n, gain_ref, wg, mg, sg, wu, mu, su, out_gate, out_up, col_gate, col_up,
    values, moments, squares, ready, parts, in_sem, own_sem, part_send, part_recv, send_sem, recv_sem,
):
    me = lax.axis_index("rows")
    w = lax.axis_index("width")
    length = n // 2
    place, side = me // 2, me % 2
    mate = place + 1 - 2 * (place % 2)
    rows, columns = wg.shape
    cuts = column_cuts(columns)
    half = len(cuts)
    chunks = [(t, at, size) for t in range(2) for at, size in cuts]
    sources = ((wg, mg, sg), (wu, mu, su))
    outs = (out_gate, out_up)
    cols = (col_gate, col_up)

    def fetch(k):
        t, at, size = chunks[k]
        return [
            pltpu.make_async_copy(src.at[:, pl.ds(at, size)], dst.at[t, :, pl.ds(at, size)], in_sem.at[i, k])
            for i, (src, dst) in enumerate(zip(sources[t], (values, moments, squares)))
        ]

    for k in range(len(chunks)):
        for copy in fetch(k):
            copy.start()

    barrier = pltpu.get_barrier_semaphore()

    def greet(i, carry):
        peer = lax.rem(me + i, n)
        pl.semaphore_signal(barrier, inc=1, device_id=(peer, w), device_id_type=MESH)
        return carry

    lax.fori_loop(1, n, greet, 0)

    def part_copy(k, peer):
        t, at, size = chunks[k]
        here = parts.at[me, t, :, pl.ds(at, size)]
        return pltpu.make_async_remote_copy(
            src_ref=here, dst_ref=here, send_sem=part_send.at[k], recv_sem=part_recv.at[k],
            device_id=(peer, w), device_id_type=MESH,
        )

    def compute(k):
        t, at, size = chunks[k]
        for copy in fetch(k):
            copy.wait()

        def step(b, total):
            here = pl.ds(pl.multiple_of(b * block_rows, block_rows), block_rows)
            there = pl.ds(at, size)
            weight = values[t, here, there]
            latest = weight - learn_rate * (
                moments[t, here, there] / (jnp.sqrt(squares[t, here, there]) + tiny_value) + decay_rate * weight
            )
            gain = jnp.concatenate([gain_ref[here, :]] * (size // lanes), axis=1)
            gained = latest * gain
            values[t, here, there] = gained
            squared = gained * gained
            for r in range(0, block_rows, 8):
                total = total + squared[r : r + 8]
            return total

        total = lax.fori_loop(0, rows // block_rows, step, jnp.zeros((8, size), jnp.float32))
        parts[me, t, :, pl.ds(at, size)] = jnp.sum(total, axis=0, keepdims=True)

    def share_parts(k):
        def send(i, carry):
            part_copy(k, lax.rem(me + i, n)).start()
            return carry

        lax.fori_loop(1, n, send, 0)

    def part_bytes(k, sem):
        t, at, size = chunks[k]
        refs = parts.at[pl.ds(0, n - 1), t, :, pl.ds(at, size)]
        return pltpu.make_async_copy(refs, refs, sem)

    def block(share, k):
        t, at, size = chunks[k]
        start = pl.multiple_of(share * rows, rows)
        return outs[t].at[pl.ds(start, rows), pl.ds(at, size)]

    own_slot = 0

    def own(k):
        t, at, size = chunks[k]
        return ready.at[t, :, pl.ds(at, size)]

    def keep(k):
        return pltpu.make_async_copy(own(k), block(me, k), own_sem.at[k])

    def push(link, slot, share, k):
        there = ((place - 1) * 2 + side, (place + 1) * 2 + side, place * 2 + 1 - side)[link]
        here = block(share, k)
        return pltpu.make_async_remote_copy(
            src_ref=own(k) if slot is own_slot else here, dst_ref=here,
            send_sem=send_sem.at[link, slot, k], recv_sem=recv_sem.at[share, k],
            device_id=(there, w), device_id_type=MESH,
        )

    def arrived(share, k):
        here = block(share, k)
        pltpu.make_async_copy(here, here, recv_sem.at[share, k]).wait()

    def finish(k):
        t, at, size = chunks[k]
        part_bytes(k, part_recv.at[k]).wait()
        total = parts[0, t, :, pl.ds(at, size)]
        for i in range(1, n):
            total = total + parts[i, t, :, pl.ds(at, size)]
        scale = jnp.sqrt(total)
        cols[t][:, pl.ds(at, size)] = scale

        def step(b, carry):
            here = pl.ds(pl.multiple_of(b * block_rows, block_rows), block_rows)
            ready[t, here, pl.ds(at, size)] = (values[t, here, pl.ds(at, size)] / scale).astype(jnp.bfloat16)
            return carry

        lax.fori_loop(0, rows // block_rows, step, 0)

    def send_own(k):
        @pl.when(place > 0)
        def _():
            push(0, 0, me, k).start()

        @pl.when(place < length - 1)
        def _():
            push(1, 0, me, k).start()

        push(2, 0, me, k).start()
        keep(k).start()

    compute(0)
    pl.semaphore_wait(barrier, n - 1)
    share_parts(0)
    for k in range(len(chunks)):
        if k + 1 < len(chunks):
            compute(k + 1)
            share_parts(k + 1)
        finish(k)
        send_own(k)

    def spread(d, carry):
        for k in range(len(chunks)):
            @pl.when(place + d < length)
            def _():
                share = (place + d) * 2 + side
                arrived(share, k)

                @pl.when(place > 0)
                def _():
                    push(0, d, share, k).start()

                if k < half:
                    push(2, d, share, k).start()
                else:
                    @pl.when(place + d != mate)
                    def _():
                        push(2, d, share, k).start()

            @pl.when(place - d >= 0)
            def _():
                share = (place - d) * 2 + side
                arrived(share, k)

                @pl.when(place < length - 1)
                def _():
                    push(1, d, share, k).start()

                if k < half:
                    push(2, length + d, share, k).start()
                else:
                    @pl.when(place - d != mate)
                    def _():
                        push(2, length + d, share, k).start()

        return carry

    def extra(action):
        share = place * 2 + 1 - side
        for k in range(half, len(chunks)):
            if action == "start":
                arrived(share, k)

            @pl.when(mate < place)
            def _():
                copy = push(0, length, share, k)
                copy.start() if action == "start" else copy.wait_send()

            @pl.when(mate > place)
            def _():
                copy = push(1, length, share, k)
                copy.start() if action == "start" else copy.wait_send()

    middle = max(1, length // 2) + 1
    lax.fori_loop(1, middle, spread, 0)
    extra("start")
    lax.fori_loop(middle, length, spread, 0)

    def collect(q, carry):
        share = q * 2 + 1 - side
        for k in range(len(chunks)):
            if k < half:
                arrived(share, k)
            else:
                @pl.when(q != place)
                def _():
                    arrived(share, k)
        return carry

    lax.fori_loop(0, length, collect, 0)

    for k in range(len(chunks)):
        part_bytes(k, part_send.at[k]).wait()
        keep(k).wait()

        @pl.when(place > 0)
        def _():
            push(0, 0, me, k).wait_send()

        @pl.when(place < length - 1)
        def _():
            push(1, 0, me, k).wait_send()

        push(2, 0, me, k).wait_send()
    extra("wait")

    def drain(d, carry):
        for k in range(len(chunks)):
            @pl.when(place + d < length)
            def _():
                share = (place + d) * 2 + side

                @pl.when(place > 0)
                def _():
                    push(0, d, share, k).wait_send()

                if k < half:
                    push(2, d, share, k).wait_send()
                else:
                    @pl.when(place + d != mate)
                    def _():
                        push(2, d, share, k).wait_send()

            @pl.when(place - d >= 0)
            def _():
                share = (place - d) * 2 + side

                @pl.when(place < length - 1)
                def _():
                    push(1, d, share, k).wait_send()

                if k < half:
                    push(2, length + d, share, k).wait_send()
                else:
                    @pl.when(place - d != mate)
                    def _():
                        push(2, length + d, share, k).wait_send()

        return carry

    lax.fori_loop(1, length, drain, 0)


def per_device(n, weight_gate, moment_gate, square_gate, weight_up, moment_up, square_up, norm_gain):
    rows, columns = weight_gate.shape
    gain = jnp.broadcast_to(norm_gain[:, None], (rows, lanes))
    count = 2 * len(column_cuts(columns))
    vmem = pl.BlockSpec(memory_space=pltpu.VMEM)
    hbm = pl.BlockSpec(memory_space=pltpu.HBM)
    scratch_bytes = 7 * rows * columns * 4
    ready_gate, ready_up, column_gate, column_up = pl.pallas_call(
        functools.partial(gather_kernel, n),
        out_shape=(
            jax.ShapeDtypeStruct((n * rows, columns), jnp.bfloat16),
            jax.ShapeDtypeStruct((n * rows, columns), jnp.bfloat16),
            jax.ShapeDtypeStruct((1, columns), jnp.float32),
            jax.ShapeDtypeStruct((1, columns), jnp.float32),
        ),
        in_specs=[vmem] + [hbm] * 6,
        out_specs=(hbm, hbm, vmem, vmem),
        scratch_shapes=[
            pltpu.VMEM((2, rows, columns), jnp.float32),
            pltpu.VMEM((2, rows, columns), jnp.float32),
            pltpu.VMEM((2, rows, columns), jnp.float32),
            pltpu.VMEM((2, rows, columns), jnp.bfloat16),
            pltpu.VMEM((n, 2, 1, columns), jnp.float32),
            pltpu.SemaphoreType.DMA((3, count)),
            pltpu.SemaphoreType.DMA((count,)),
            pltpu.SemaphoreType.DMA((count,)),
            pltpu.SemaphoreType.DMA((count,)),
            pltpu.SemaphoreType.DMA((3, n, count)),
            pltpu.SemaphoreType.DMA((n, count)),
        ],
        compiler_params=pltpu.CompilerParams(
            collective_id=0, has_side_effects=True, vmem_limit_bytes=scratch_bytes + 8 * 2**20
        ),
        name="step_and_gather",
    )(gain, weight_gate, moment_gate, square_gate, weight_up, moment_up, square_up)
    return ready_gate, ready_up, column_gate.reshape(columns), column_up.reshape(columns)


def solution(mesh):
    split = P("rows", "width")
    return jax.shard_map(
        functools.partial(per_device, mesh.shape["rows"]),
        mesh=mesh,
        in_specs=(split,) * 6 + (P("rows"),),
        out_specs=(P(None, "width"), P(None, "width"), P("width"), P("width")),
        check_vma=False,
    )
```

time: 431 us -> 281 us (0.65)
  waiting for transfers between devices: 346 us -> 0 us
  Pallas kernels: 0 us -> 249 us
  blocking collectives: 38.8 us -> 0 us
  between operations: 14.1 us -> 0.66 us
  other arithmetic: 13.9 us -> 1.26 us
  local copies, waits for them, and re-layouts: 17.5 us -> 29.6 us
    all_gather x2 -> x0, waiting for transfers between devices: 346 us -> none  [the longest x1 175 us: per_device(): lax.all_gather(narrow_up, 'rows', axis=0, tiled=True)]
    pallas_call x0 -> x1, Pallas kernels: none -> 249 us  [per_device(): pl.pallas_call(functools.partial(gather_kernel, n), out_shape=(jax.ShapeD...]
    psum x1 -> x0, blocking collectives: 38.8 us -> none  [per_device(): lax.psum((jnp.sum(latest_gained_gate * latest_gained_gate, axis=0), jnp.s...]
    unnamed x8 -> x16, local copies, waits for them, and re-layouts: 17.5 us -> 28.8 us
    reduce_sum x1 -> x0, other arithmetic: 9.34 us -> none  [per_device(): jnp.sum(latest_gained_up * latest_gained_up, axis=0)]
    convert_element_type x2 -> x0, other arithmetic: 4.53 us -> none  [the longest x1 3.21 us: per_device(): (latest_gained_gate / column_gate).astype(jnp.bfloat16)]
  transfers between devices with their start and end apart: 2 -> 0, of which waited for: 2 -> 0; matrix products, arithmetic and copies ran while one was open for 0% -> 0% of each run, Pallas kernels for 0% -> 0%
where the time goes in v1:
time: 281 us
  Pallas kernels  249 us (89%)
  local copies, waits for them, and re-layouts  29.6 us (11%)
    pallas_call x1, Pallas kernels, per_device(): pl.pallas_call(functools.partial(gather_kernel, n), out_shape=(jax.ShapeD...  249 us
    unnamed x16, local copies, waits for them, and re-layouts  28.8 us

profile of v1, /device:TPU:0, one launch (start us, length us, event | category | flops | bytes accessed | tf_op | source)
XLA Modules:
  0.0 280.9 jit_solution(9838964107342390650)
XLA Ops:
  0.6 0.8 broadcast_in_dim.2.gain_ref
  1.4 0.0 copy-start
  1.4 1.9 copy-done
  3.3 0.0 copy-start.1
  3.3 1.9 copy-done.1
  5.2 0.0 copy-start.2
  5.2 1.9 copy-done.2
  7.1 0.0 copy-start.3
  7.1 1.9 copy-done.3
  8.9 0.0 copy-start.4
  8.9 1.9 copy-done.4
  10.8 0.0 copy-start.5
  10.8 1.9 copy-done.5
  12.7 249.4 %step_and_gather.1 = (bf16[2560,2432]{1,0:T(8,128)(2,1)}, bf16[2560,2432]{1,0:T(8,128)(2,1)}, f32[1,2432]{1,0:T(1,128)S(1)}, f32[1,2432]{1,0:T(1,128)S(1)}) custom-call(f32[320,128]{1,0:T(8,128)S(1)} %broadcast_in_dim.2.gain_ref, f32[320,2432]{1,0:T(8,128)S(1)} %copy-done, f32[320,2432]{1,0:T(8,128)S(1)} %copy-done.1, f32[320,2432]{1,0:T(8,128)S(1)} %copy-done.2, ...), custom_call_target="tpu_custom_call" | custom-call | tf_op jit(solution)/shard_map/step_and_gather/pallas_call | solution.py:305
  262.1 0.6 reduce
  262.7 0.6 reduce.1
  263.4 0.0 copy-start.6
  263.4 11.0 %copy.13 = bf16[2560,2432]{1,0:T(8,128)(2,1)} copy(bf16[2560,2432]{1,0:T(8,128)(2,1)} %get-tuple-element.16) | data formatting | bytes 24903680
  274.4 1.8 copy-done.6
  276.1 4.7 %copy.14 = bf16[2560,2432]{1,0:T(8,128)(2,1)} copy(bf16[2560,2432]{1,0:T(8,128)(2,1)S(1)} %copy-done.6) | data formatting | bytes 24903680
Async XLA Ops:
  1.4 1.9 copy-start
  3.3 1.9 copy-start.1
  5.2 1.9 copy-start.2
  7.1 1.9 copy-start.3
  8.9 1.9 copy-start.4
  10.8 1.9 copy-start.5
  263.4 12.8 %copy-start.6 = (bf16[2560,2432]{1,0:T(8,128)(2,1)S(1)}, bf16[2560,2432]{1,0:T(8,128)(2,1)}, u32[]{:S(2)}) copy-start(bf16[2560,2432]{1,0:T(8,128)(2,1)} %get-tuple-element.17) | copy-start | bytes 37355524

commit v2 on v1

--- a/solution.py
+++ b/solution.py
@@ -11,6 +11,7 @@
 decay_rate = 0.1
 tiny_value = 1e-08
 lanes = 128
+vmem_bytes = 67043328
 block_rows = 16
 MESH = pl.DeviceIdType.MESH
 
@@ -30,7 +31,7 @@
 
 def gather_kernel(
     n, gain_ref, wg, mg, sg, wu, mu, su, out_gate, out_up, col_gate, col_up,
-    values, moments, squares, ready, parts, in_sem, own_sem, part_send, part_recv, send_sem, recv_sem,
+    values, moments, squares, parts, in_sem, part_send, part_recv, send_sem, recv_sem,
 ):
     me = lax.axis_index("rows")
     w = lax.axis_index("width")
@@ -113,20 +114,11 @@
         start = pl.multiple_of(share * rows, rows)
         return outs[t].at[pl.ds(start, rows), pl.ds(at, size)]
 
-    own_slot = 0
-
-    def own(k):
-        t, at, size = chunks[k]
-        return ready.at[t, :, pl.ds(at, size)]
-
-    def keep(k):
-        return pltpu.make_async_copy(own(k), block(me, k), own_sem.at[k])
-
     def push(link, slot, share, k):
         there = ((place - 1) * 2 + side, (place + 1) * 2 + side, place * 2 + 1 - side)[link]
         here = block(share, k)
         return pltpu.make_async_remote_copy(
-            src_ref=own(k) if slot is own_slot else here, dst_ref=here,
+            src_ref=here, dst_ref=here,
             send_sem=send_sem.at[link, slot, k], recv_sem=recv_sem.at[share, k],
             device_id=(there, w), device_id_type=MESH,
         )
@@ -146,7 +138,8 @@
 
         def step(b, carry):
             here = pl.ds(pl.multiple_of(b * block_rows, block_rows), block_rows)
-            ready[t, here, pl.ds(at, size)] = (values[t, here, pl.ds(at, size)] / scale).astype(jnp.bfloat16)
+            there = pl.ds(pl.multiple_of(me * rows + b * block_rows, block_rows), block_rows)
+            outs[t][there, pl.ds(at, size)] = (values[t, here, pl.ds(at, size)] / scale).astype(jnp.bfloat16)
             return carry
 
         lax.fori_loop(0, rows // block_rows, step, 0)
@@ -161,7 +154,6 @@
             push(1, 0, me, k).start()
 
         push(2, 0, me, k).start()
-        keep(k).start()
 
     compute(0)
     pl.semaphore_wait(barrier, n - 1)
@@ -245,7 +237,6 @@
 
     for k in range(len(chunks)):
         part_bytes(k, part_send.at[k]).wait()
-        keep(k).wait()
 
         @pl.when(place > 0)
         def _():
@@ -295,41 +286,67 @@
     lax.fori_loop(1, length, drain, 0)
 
 
+def write_kernel(pieces, gate, up, out_gate, out_up, sem):
+    step = gate.shape[0] // pieces
+    copies = [
+        pltpu.make_async_copy(src.at[pl.ds(i * step, step)], dst.at[pl.ds(i * step, step)], sem.at[t, i])
+        for i in range(pieces)
+        for t, (src, dst) in enumerate(((gate, out_gate), (up, out_up)))
+    ]
+    for copy in copies:
+        copy.start()
+    for copy in copies:
+        copy.wait()
+
+
+def write_out(pieces, gate, up):
+    vmem = pl.BlockSpec(memory_space=pltpu.VMEM)
+    hbm = pl.BlockSpec(memory_space=pltpu.HBM)
+    return pl.pallas_call(
+        functools.partial(write_kernel, pieces),
+        out_shape=[jax.ShapeDtypeStruct(a.shape, a.dtype) for a in (gate, up)],
+        in_specs=[vmem, vmem],
+        out_specs=[hbm, hbm],
+        scratch_shapes=[pltpu.SemaphoreType.DMA((2, pieces))],
+        compiler_params=pltpu.CompilerParams(vmem_limit_bytes=2**20),
+        name="write_out",
+    )(gate, up)
+
+
 def per_device(n, weight_gate, moment_gate, square_gate, weight_up, moment_up, square_up, norm_gain):
     rows, columns = weight_gate.shape
     gain = jnp.broadcast_to(norm_gain[:, None], (rows, lanes))
     count = 2 * len(column_cuts(columns))
     vmem = pl.BlockSpec(memory_space=pltpu.VMEM)
     hbm = pl.BlockSpec(memory_space=pltpu.HBM)
-    scratch_bytes = 7 * rows * columns * 4
+    room = vmem_bytes - 2 * n * rows * columns * 2 - 3 * 2**19
     ready_gate, ready_up, column_gate, column_up = pl.pallas_call(
         functools.partial(gather_kernel, n),
         out_shape=(
-            jax.ShapeDtypeStruct((n * rows, columns), jnp.bfloat16),
-            jax.ShapeDtypeStruct((n * rows, columns), jnp.bfloat16),
+            pltpu.VMEM((n * rows, columns), jnp.bfloat16),
+            pltpu.VMEM((n * rows, columns), jnp.bfloat16),
             jax.ShapeDtypeStruct((1, columns), jnp.float32),
             jax.ShapeDtypeStruct((1, columns), jnp.float32),
         ),
         in_specs=[vmem] + [hbm] * 6,
-        out_specs=(hbm, hbm, vmem, vmem),
+        out_specs=(vmem, vmem, vmem, vmem),
         scratch_shapes=[
             pltpu.VMEM((2, rows, columns), jnp.float32),
             pltpu.VMEM((2, rows, columns), jnp.float32),
             pltpu.VMEM((2, rows, columns), jnp.float32),
-            pltpu.VMEM((2, rows, columns), jnp.bfloat16),
             pltpu.VMEM((n, 2, 1, columns), jnp.float32),
             pltpu.SemaphoreType.DMA((3, count)),
-            pltpu.SemaphoreType.DMA((count,)),
             pltpu.SemaphoreType.DMA((count,)),
             pltpu.SemaphoreType.DMA((count,)),
             pltpu.SemaphoreType.DMA((3, n, count)),
             pltpu.SemaphoreType.DMA((n, count)),
         ],
         compiler_params=pltpu.CompilerParams(
-            collective_id=0, has_side_effects=True, vmem_limit_bytes=scratch_bytes + 8 * 2**20
+            collective_id=0, has_side_effects=True, vmem_limit_bytes=room
         ),
         name="step_and_gather",
     )(gain, weight_gate, moment_gate, square_gate, weight_up, moment_up, square_up)
+    ready_gate, ready_up = write_out(n, ready_gate, ready_up)
     return ready_gate, ready_up, column_gate.reshape(columns), column_up.reshape(columns)
 
 

time: 281 us -> 262 us (0.932)
  local copies, waits for them, and re-layouts: 29.6 us -> 1.46 us
  Pallas kernels: 249 us -> 258 us
    unnamed x16 -> x4, local copies, waits for them, and re-layouts: 28.8 us -> 0.01 us
    pallas_call x1 -> x2, Pallas kernels: 249 us -> 258 us  [the longest x1 250 us: per_device(): pl.pallas_call(functools.partial(gather_kernel, n), out_shape=(pltpu.VMEM...]
where the time goes in v2:
time: 262 us
  Pallas kernels  258 us (98%)
    pallas_call x1, Pallas kernels, per_device(): pl.pallas_call(functools.partial(gather_kernel, n), out_shape=(pltpu.VMEM...  250 us
    pallas_call x1, Pallas kernels, write_out(): pl.pallas_call(functools.partial(write_kernel, pieces), out_shape=[jax.Sh...  8.43 us

profile of v2, /device:TPU:0, one launch (start us, length us, event | category | flops | bytes accessed | tf_op | source)
XLA Modules:
  0.0 261.5 jit_solution(3788356689067105910)
XLA Ops:
  0.6 1.5 broadcast_in_dim.2.gain_ref
  2.1 249.7 %step_and_gather.1 = (bf16[2560,2432]{1,0:T(8,128)(2,1)S(1)}, bf16[2560,2432]{1,0:T(8,128)(2,1)S(1)}, f32[1,2432]{1,0:T(1,128)}, f32[1,2432]{1,0:T(1,128)}) custom-call(f32[320,128]{1,0:T(8,128)} %broadcast_in_dim.2.gain_ref, f32[320,2432]{1,0:T(8,128)} %wg.1, f32[320,2432]{1,0:T(8,128)} %mg.1, f32[320,2432]{1,0:T(8,128)} %sg.1, f32[320,2432]{1,0:T(8,128)} %wu.1, ...), custom_call_target="tpu_custom_call" | custom-call | tf_op jit(solution)/shard_map/step_and_gather/pallas_call | solution.py:323
  251.8 0.0 copy-start.1
  251.8 0.0 copy-start
  251.8 8.4 %write_out.1 = (bf16[2560,2432]{1,0:T(8,128)(2,1)}, bf16[2560,2432]{1,0:T(8,128)(2,1)}) custom-call(bf16[2560,2432]{1,0:T(8,128)(2,1)S(1)} %get-tuple-element.10.gate, bf16[2560,2432]{1,0:T(8,128)(2,1)S(1)} %get-tuple-element.11.up), custom_call_target="tpu_custom_call" | custom-call | tf_op jit(solution)/shard_map/write_out/pallas_call | solution.py:305
  260.2 0.0 copy-done.1
  260.2 0.6 reduce
  260.9 0.0 copy-done
  260.9 0.6 reduce.1
Async XLA Ops:
  251.8 8.5 %copy-start.1 = (f32[1,2432]{1,0:T(1,128)S(1)}, f32[1,2432]{1,0:T(1,128)}, u32[]{:S(2)}) copy-start(f32[1,2432]{1,0:T(1,128)} %get-tuple-element.14) | copy-start | bytes 29188
  251.8 9.1 %copy-start = (f32[1,2432]{1,0:T(1,128)S(1)}, f32[1,2432]{1,0:T(1,128)}, u32[]{:S(2)}) copy-start(f32[1,2432]{1,0:T(1,128)} %get-tuple-element.15) | copy-start | bytes 29188
